TPU v7x, 32 devices: a whole 2x2x4 slice. The times are simulated.
32 devices in a mesh: groups: 2 (over y), ctx: 8 (over z, x), col: 2 (over core).
Axes of the slice: x: 2, y: 2, z: 4, core: 2. Of those that a mesh axis runs over, the one named last changes fastest.
Arguments:
- activations: bfloat16 [2048, 4096], P(('groups', 'ctx'), 'col'), parts along dimension 0, may hold values from -6 to 6
- gradients: bfloat16 [2048, 14336], P(('groups', 'ctx'), 'col'), parts along dimension 0, may hold values from -6 to 6
- doc_ids: int32 [2048], P(('groups', 'ctx')), parts along dimension 0, may hold values from 0 to 11, as said below
- proj_in: bfloat16 [4096, 64], P('col'), may hold values from -0.046875 to 0.046875
- proj_out: bfloat16 [14336, 64], P('col'), may hold values from -0.0234375 to 0.0234375
- inverse: float32 [4096, 4096], P('col', 'ctx')
- store_rows: bfloat16 [2048, 4096], P(('groups', 'ctx', 'col')), parts along dimension 0, may hold values from -0.09375 to 0.09375
Outputs:
- scores: float32 [12, 2048], P(None, ('groups', 'ctx', 'col')), parts along dimension 1
There are 2 independent parts, one for each index of `groups`. A program takes and returns all parts, laid end to end along the dimension named above; an argument that names none is the same for every part. Nothing has to cross between parts.
Inputs may be any that keep to these rules, and one draw needn't show every extreme that they name: `doc_ids`: document numbers never fall and rise by at most one from a token to the next, starting at 0. Every aligned block of 128 tokens holds the last token of one or two documents; the last token of the sequence ends document 12 - 1.
All inputs are finite; a program needn't handle non-finite values.
Results may differ from a plain program's by a relative error of at most 0.0029.
Values may be sent and summed in bfloat16 or wider, within the bound.
A program may use at most 64 MiB of HBM per device.

v0:
```python
import functools

import jax
import jax.numpy as jnp
from jax import lax
from jax.experimental import pallas as pl
from jax.experimental.pallas import tpu as pltpu
from jax.sharding import PartitionSpec as P


def from_behind(block, axis, distance):
    devices = range(lax.axis_size(axis))
    route = [(i - distance, i) for i in devices if i - distance in devices]
    return lax.ppermute(block, axis, route)


def shards(activations, gradients, doc_ids, proj_in, proj_out, inverse, store_rows):
    left_part = jnp.dot(activations, proj_in, preferred_element_type=jnp.float32)
    right_part = jnp.dot(gradients, proj_out, preferred_element_type=jnp.float32)
    proj_left, proj_right = lax.psum((left_part, right_part), "col")
    proj_rank = proj_right.shape[1]
    half_rank = proj_rank // lax.axis_size("col")
    own_half = lax.dynamic_slice_in_dim(proj_left, lax.axis_index("col") * half_rank, half_rank, 1)
    first_doc = doc_ids[0]
    slot_index = doc_ids - first_doc
    onehot = (slot_index[:, None] == jnp.arange(3, dtype=jnp.int32)[None, :]).astype(jnp.float32)
    weighted = (onehot[:, :, None] * own_half[:, None, :]).reshape(own_half.shape[0], 3 * half_rank)
    local_sums = lax.dot_general(
        weighted,
        proj_right,
        (((0,), (0,)), ((), ())),
        precision=lax.Precision.HIGHEST,
        preferred_element_type=jnp.float32,
    ).reshape(3, half_rank * proj_rank)
    doc_count = 3 * lax.axis_size("ctx") // 2
    last_row = lax.dynamic_index_in_dim(local_sums, slot_index[-1], 0, keepdims=False)
    incoming, incoming_id = from_behind((last_row, doc_ids[-1].astype(jnp.float32)), "ctx", 1)
    matches = (incoming_id == first_doc.astype(jnp.float32)).astype(jnp.float32)
    head_row = local_sums[0] + matches * incoming
    owned_rows = jnp.stack([head_row, local_sums[1]])
    owned_ids = (first_doc + jnp.arange(2, dtype=jnp.int32)).astype(jnp.float32)
    gathered, gathered_ids = (
        lax.all_gather(owned_rows, "ctx", axis=0, tiled=True),
        lax.all_gather(owned_ids, "ctx", axis=0, tiled=True),
    )
    positions = jnp.arange(gathered.shape[0], dtype=jnp.int32)
    wanted = jnp.arange(doc_count, dtype=jnp.int32).astype(jnp.float32)
    found = gathered_ids[None, :] == wanted[:, None]
    chosen = jnp.max(jnp.where(found, positions[None, :], -1), axis=1)
    doc_grads = jnp.take(gathered, chosen, axis=0)
    partial_q = jnp.dot(
        doc_grads, inverse, precision=lax.Precision.HIGHEST, preferred_element_type=jnp.float32
    )
    precond = lax.psum(partial_q, "col").astype(jnp.bfloat16)
    return lax.dot_general(
        lax.all_gather(precond, "ctx", axis=1, tiled=True),
        store_rows,
        (((1,), (1,)), ((), ())),
        preferred_element_type=jnp.float32,
    )


LANES = 128
SLOTS = 3
CHUNKS = 4
MESH = pl.DeviceIdType.MESH
def sums_order(n):
    order = []
    for r in range(1, n // 2 + 1):
        order += [n - r, r] if n - r != r else [r]
    return order


NT = (((1,), (1,)), ((), ()))


def halves(value):
    high = value.astype(jnp.bfloat16).astype(jnp.float32)
    return high, value - high


def dot_nt(left, right):
    return lax.dot_general(left, right, NT, preferred_element_type=jnp.float32)


def score_kernel(
    n, cols, docs,
    act, grad, ids, pin, pout, inv, store, out,
    act_v, grad_v, pin_v, pout_v, inv_v, store_v, inv_hi, inv_lo,
    store_t, ids_all, part_l, part_r, from_l, from_r, full_l, sums, q_part, q_from, q_all,
    load_sem, ids_send, ids_recv, pair_send, pair_recv, sums_send, sums_recv, q_send, q_recv,
):
    me = lax.axis_index("ctx")
    core = lax.axis_index("col")
    other = cols - 1 - core
    rank = pin.shape[0]
    half = rank // cols
    pack = LANES // rank
    groups = half // pack
    piece = SLOTS * groups
    width = q_part.shape[2]

    loads = [
        pltpu.make_async_copy(ids, ids_all.at[me], load_sem.at[0]),
        pltpu.make_async_copy(act, act_v, load_sem.at[1]),
        pltpu.make_async_copy(pin, pin_v, load_sem.at[2]),
    ]
    step = grad.shape[1] // CHUNKS
    for i in range(CHUNKS):
        span = pl.ds(i * step, step)
        loads.append(pltpu.make_async_copy(pout.at[:, span], pout_v.at[:, span], load_sem.at[3 + 2 * i]))
        loads.append(pltpu.make_async_copy(grad.at[:, span], grad_v.at[:, span], load_sem.at[4 + 2 * i]))
    loads.append(pltpu.make_async_copy(inv, inv_v, load_sem.at[3 + 2 * CHUNKS]))
    loads.append(pltpu.make_async_copy(store, store_v, load_sem.at[4 + 2 * CHUNKS]))
    for load in loads:
        load.start()

    barrier = pltpu.get_barrier_semaphore()
    ctx_peers = {r: {"ctx": jnp.bitwise_xor(me, r)} for r in sums_order(n)}
    peers = {}
    for r in range(n):
        for d in range(cols):
            if r or d:
                peers[cols * r + d] = {"ctx": lax.rem(me + r, n), "col": jnp.bitwise_xor(core, d)}
    for peer in peers.values():
        pl.semaphore_signal(barrier, inc=1, device_id=peer, device_id_type=MESH)

    loads[1].wait()
    loads[2].wait()
    part_l[...] = dot_nt(pin_v[...], act_v[...])

    def remote(src, dst, send, recv, peer):
        copy = pltpu.make_async_remote_copy(
            src_ref=src, dst_ref=dst, send_sem=send, recv_sem=recv, device_id=peer, device_id_type=MESH
        )
        copy.start()
        return copy

    right = None
    for i in range(CHUNKS):
        span = pl.ds(i * step, step)
        loads[3 + 2 * i].wait()
        loads[4 + 2 * i].wait()
        term = dot_nt(pout_v[:, span], grad_v[:, span])
        right = term if right is None else right + term
    part_r[...] = right
    pl.semaphore_wait(barrier, len(peers))
    partner = {"col": other}
    copy_l = remote(part_l.at[pl.ds(other * half, half)], from_l, pair_send.at[0], pair_recv.at[0], partner)
    copy_r = remote(part_r, from_r, pair_send.at[1], pair_recv.at[1], partner)
    ids_copies = [
        remote(ids, ids_all.at[me], ids_send.at[r], ids_recv.at[r], ctx_peers[r])
        for r in ctx_peers
    ]

    loads[0].wait()
    own_ids = ids_all[me]
    first = own_ids[:, 0:1]
    masks = [(own_ids == first + s).astype(jnp.float32) for s in range(SLOTS)]
    copy_l.wait_recv()
    full_l[...] = part_l[pl.ds(pl.multiple_of(core * half, half), half), :] + from_l[...]
    highs, lows = [], []
    for p in range(pack):
        rows = full_l[pl.ds(p, groups, stride=pack), :]
        high, low = halves(jnp.concatenate([rows * mask for mask in masks], axis=0))
        highs.append(high)
        lows.append(low)
    weights = jnp.concatenate(highs + highs + lows, axis=1).astype(jnp.bfloat16)
    copy_r.wait_recv()
    high, low = halves(part_r[...] + from_r[...])
    zero = jnp.zeros_like(high)

    def diagonal(block, p):
        return [block if q == p else zero for q in range(pack)]

    spread = jnp.concatenate(
        [
            jnp.concatenate(diagonal(high, p) + diagonal(low, p) + diagonal(high, p), axis=1)
            for p in range(pack)
        ],
        axis=0,
    ).astype(jnp.bfloat16)
    mine = pl.ds(pl.multiple_of(me * piece, 8), piece)
    sums[mine, :] = dot_nt(weights, spread)
    sums_copies = [
        remote(sums.at[mine], sums.at[mine], sums_send.at[r], sums_recv.at[r], ctx_peers[r])
        for r in ctx_peers
    ]

    loads[3 + 2 * CHUNKS].wait()
    band = LANES

    def split(i, carry):
        rows = pl.ds(pl.multiple_of(i * band, band), band)
        high, low = halves(inv_v[rows, :])
        inv_hi[rows, :] = high.astype(jnp.bfloat16)
        inv_lo[rows, :] = low.astype(jnp.bfloat16)
        return carry

    lax.fori_loop(0, inv_v.shape[0] // band, split, 0)
    loads[4 + 2 * CHUNKS].wait()
    store_t[...] = store_v[...].T

    for copy in ids_copies:
        copy.wait_recv()
    doc_rows = q_part.shape[1]
    column = lax.broadcasted_iota(jnp.int32, (1, SLOTS * n), 1)
    doc_of = jnp.zeros((1, SLOTS * n), jnp.int32)
    for b in range(n):
        inside = (column >= b * SLOTS) & (column < (b + 1) * SLOTS)
        doc_of = jnp.where(inside, ids_all[b][:, 0:1] + (column - b * SLOTS), doc_of)
    pick = (lax.broadcasted_iota(jnp.int32, (doc_rows, SLOTS * n), 0) == doc_of).astype(jnp.float32)

    for copy in sums_copies:
        copy.wait_recv()
    gathered = jnp.concatenate(
        [sums[pl.ds(k, SLOTS * n, stride=groups), :] for k in range(groups)], axis=1
    )
    high, low = halves(gathered)
    both = jnp.concatenate([high, low], axis=0).astype(jnp.bfloat16)
    main = jnp.dot(both, inv_hi[...], preferred_element_type=jnp.float32)
    rest = jnp.dot(high.astype(jnp.bfloat16), inv_lo[...], preferred_element_type=jnp.float32)
    rows = main[: SLOTS * n] + main[SLOTS * n :] + rest
    picked = jnp.dot(pick, rows, precision=lax.Precision.HIGHEST, preferred_element_type=jnp.float32)
    for c in range(cols):
        q_part[c] = picked[:, c * width : (c + 1) * width]
    copy_q = remote(q_part.at[other], q_from, pair_send.at[2], pair_recv.at[2], partner)
    copy_q.wait_recv()
    slot = me * cols + core
    q_all[slot] = (q_part[core] + q_from[...]).astype(jnp.bfloat16)
    q_copies = [
        remote(q_all.at[slot], q_all.at[slot], q_send.at[i], q_recv.at[i], peers[i])
        for i in peers
    ]
    for copy in q_copies:
        copy.wait_recv()
    precond = jnp.concatenate([q_all[i] for i in range(n * cols)], axis=1)
    out[...] = jnp.dot(precond, store_t[...], preferred_element_type=jnp.float32)[:docs]
    for copy in [copy_l, copy_r, copy_q] + ids_copies + sums_copies + q_copies:
        copy.wait_send()


def fused(n, cols, activations, gradients, doc_ids, proj_in, proj_out, inverse, store_rows):
    tokens = activations.shape[0]
    rank = proj_in.shape[1]
    half = rank // cols
    docs = SLOTS * n // 2
    doc_rows = -(-docs // 16) * 16
    width = inverse.shape[1] // cols
    piece = SLOTS * half * rank // LANES
    anywhere = pl.BlockSpec(memory_space=pl.ANY)
    dma = pltpu.SemaphoreType.DMA
    return pl.pallas_call(
        functools.partial(score_kernel, n, cols, docs),
        name="scores",
        out_shape=jax.ShapeDtypeStruct((docs, store_rows.shape[0]), jnp.float32),
        in_specs=[anywhere] * 7,
        out_specs=pl.BlockSpec(memory_space=pltpu.VMEM),
        scratch_shapes=[
            pltpu.VMEM(activations.shape, jnp.bfloat16),
            pltpu.VMEM(gradients.shape, jnp.bfloat16),
            pltpu.VMEM(proj_in.shape[::-1], jnp.bfloat16),
            pltpu.VMEM(proj_out.shape[::-1], jnp.bfloat16),
            pltpu.VMEM(inverse.shape, jnp.float32),
            pltpu.VMEM(store_rows.shape, jnp.bfloat16),
            pltpu.VMEM(inverse.shape, jnp.bfloat16),
            pltpu.VMEM(inverse.shape, jnp.bfloat16),
            pltpu.VMEM(store_rows.shape[::-1], jnp.bfloat16),
            pltpu.VMEM((n, 1, tokens), jnp.int32),
            pltpu.VMEM((rank, tokens), jnp.float32),
            pltpu.VMEM((rank, tokens), jnp.float32),
            pltpu.VMEM((half, tokens), jnp.float32),
            pltpu.VMEM((rank, tokens), jnp.float32),
            pltpu.VMEM((half, tokens), jnp.float32),
            pltpu.VMEM((n * piece, LANES), jnp.float32),
            pltpu.VMEM((cols, doc_rows, width), jnp.float32),
            pltpu.VMEM((doc_rows, width), jnp.float32),
            pltpu.VMEM((n * cols, doc_rows, width), jnp.bfloat16),
            dma((5 + 2 * CHUNKS,)),
            dma((n,)), dma((n,)),
            dma((3,)), dma((3,)),
            dma((n,)), dma((n,)),
            dma((n * cols,)), dma((n * cols,)),
        ],
        compiler_params=pltpu.CompilerParams(
            collective_id=0, has_side_effects=True, vmem_limit_bytes=60 << 20
        ),
    )(activations, gradients, doc_ids[None, :], proj_in.T, proj_out.T, inverse, store_rows)


def suits_kernel(n, cols, activations, gradients, proj_in, inverse):
    rank = proj_in.shape[1]
    return (
        cols == 2
        and activations.shape[0] == LANES
        and LANES % rank == 0
        and (rank // cols * rank) % (8 * LANES) == 0
        and gradients.shape[1] % (CHUNKS * LANES) == 0
        and inverse.shape[1] % (cols * LANES) == 0
        and n <= 16
        and n & (n - 1) == 0
    )


def solution(mesh):
    in_specs = (
        P(("groups", "ctx"), "col"),
        P(("groups", "ctx"), "col"),
        P(("groups", "ctx")),
        P("col", None),
        P("col", None),
        P("col", "ctx"),
        P(("groups", "ctx", "col"), None),
    )
    out_specs = P(None, ("groups", "ctx", "col"))
    n, cols = mesh.shape["ctx"], mesh.shape["col"]

    def body(activations, gradients, doc_ids, proj_in, proj_out, inverse, store_rows):
        args = (activations, gradients, doc_ids, proj_in, proj_out, inverse, store_rows)
        if suits_kernel(n, cols, activations, gradients, proj_in, inverse):
            return fused(n, cols, *args)
        return shards(*args)

    return jax.shard_map(body, mesh=mesh, in_specs=in_specs, out_specs=out_specs, check_vma=False)
```

profile of v0, /device:TPU:0, one launch (start us, length us, event | category | flops | bytes accessed | tf_op | source)
XLA Modules:
  0.0 22.6 jit_solution(1774838758684189736)
XLA Ops:
  0.0 21.2 %scores.1 = f32[12,64]{1,0:T(8,128)} custom-call(bf16[128,2048]{1,0:T(8,128)(2,1)} %act.1, bf16[128,7168]{1,0:T(8,128)(2,1)} %grad.1, s32[1,128]{1,0:T(1,128)} %bitcast.5, bf16[64,2048]{1,0:T(8,128)(2,1)} %bitcast.4, bf16[64,7168]{1,0:T(8,128)(2,1)} %bitcast.3, f32[2048,512]{1,0:T(8,128)} %inv.1, bf16[64,4096]{1,0:T(8,128)(2,1)} %store.1), custom_call_target="tpu_custom_call" | custom-call | tf_op jit(solution)/shard_map/scores/pallas_call | solution.py:253
  21.3 1.3 %copy.9 = f32[12,64]{1,0:T(8,128)} copy(f32[12,64]{1,0:T(8,128)} %scores.1) | data formatting | bytes 6144
where the time goes:
time: 22.7 us; the launch traced here: 22.6 us
  Pallas kernels  21.2 us (93%)
  local copies, waits for them, and re-layouts  1.3 us (6%)
    pallas_call x1, Pallas kernels, fused(): pl.pallas_call(functools.partial(score_kernel, n, cols, docs), name='scor...  21.2 us
    unnamed x1, local copies, waits for them, and re-layouts  1.3 us

commit v1 on v0

v1 whole, which is shorter than its diff:
```python
import functools

import jax
import jax.numpy as jnp
from jax import lax
from jax.experimental import pallas as pl
from jax.experimental.pallas import tpu as pltpu
from jax.sharding import PartitionSpec as P


def from_behind(block, axis, distance):
    devices = range(lax.axis_size(axis))
    route = [(i - distance, i) for i in devices if i - distance in devices]
    return lax.ppermute(block, axis, route)


def shards(activations, gradients, doc_ids, proj_in, proj_out, inverse, store_rows):
    left_part = jnp.dot(activations, proj_in, preferred_element_type=jnp.float32)
    right_part = jnp.dot(gradients, proj_out, preferred_element_type=jnp.float32)
    proj_left, proj_right = lax.psum((left_part, right_part), "col")
    proj_rank = proj_right.shape[1]
    half_rank = proj_rank // lax.axis_size("col")
    own_half = lax.dynamic_slice_in_dim(proj_left, lax.axis_index("col") * half_rank, half_rank, 1)
    first_doc = doc_ids[0]
    slot_index = doc_ids - first_doc
    onehot = (slot_index[:, None] == jnp.arange(3, dtype=jnp.int32)[None, :]).astype(jnp.float32)
    weighted = (onehot[:, :, None] * own_half[:, None, :]).reshape(own_half.shape[0], 3 * half_rank)
    local_sums = lax.dot_general(
        weighted,
        proj_right,
        (((0,), (0,)), ((), ())),
        precision=lax.Precision.HIGHEST,
        preferred_element_type=jnp.float32,
    ).reshape(3, half_rank * proj_rank)
    doc_count = 3 * lax.axis_size("ctx") // 2
    last_row = lax.dynamic_index_in_dim(local_sums, slot_index[-1], 0, keepdims=False)
    incoming, incoming_id = from_behind((last_row, doc_ids[-1].astype(jnp.float32)), "ctx", 1)
    matches = (incoming_id == first_doc.astype(jnp.float32)).astype(jnp.float32)
    head_row = local_sums[0] + matches * incoming
    owned_rows = jnp.stack([head_row, local_sums[1]])
    owned_ids = (first_doc + jnp.arange(2, dtype=jnp.int32)).astype(jnp.float32)
    gathered, gathered_ids = (
        lax.all_gather(owned_rows, "ctx", axis=0, tiled=True),
        lax.all_gather(owned_ids, "ctx", axis=0, tiled=True),
    )
    positions = jnp.arange(gathered.shape[0], dtype=jnp.int32)
    wanted = jnp.arange(doc_count, dtype=jnp.int32).astype(jnp.float32)
    found = gathered_ids[None, :] == wanted[:, None]
    chosen = jnp.max(jnp.where(found, positions[None, :], -1), axis=1)
    doc_grads = jnp.take(gathered, chosen, axis=0)
    partial_q = jnp.dot(
        doc_grads, inverse, precision=lax.Precision.HIGHEST, preferred_element_type=jnp.float32
    )
    precond = lax.psum(partial_q, "col").astype(jnp.bfloat16)
    return lax.dot_general(
        lax.all_gather(precond, "ctx", axis=1, tiled=True),
        store_rows,
        (((1,), (1,)), ((), ())),
        preferred_element_type=jnp.float32,
    )


LANES = 128
SLOTS = 3
LEFT_CHUNKS = 1
RIGHT_CHUNKS = 4
PARTS = 1
MESH = pl.DeviceIdType.MESH
NT = (((1,), (1,)), ((), ()))


def halves(value):
    high = value.astype(jnp.bfloat16).astype(jnp.float32)
    return high, value - high


def dot_nt(left, right):
    return lax.dot_general(left, right, NT, preferred_element_type=jnp.float32)


def dot(left, right):
    return jnp.dot(left, right, preferred_element_type=jnp.float32)


def await_bytes(ref, sem):
    pltpu.make_async_copy(ref, ref, sem).wait()


def score_kernel(
    n, cols, docs,
    act, grad, ids, pin, pout, inv, store, out,
    xl, xr, inv_v, store_v, inv_hi, inv_lo, store_t, ids_all,
    part, came, full_l, sums, q_part, q_from, q_all,
    load_sem, send_sem, recv_sem,
):
    me = lax.axis_index("ctx")
    core = lax.axis_index("col")
    other = cols - 1 - core
    tokens = act.shape[0]
    rank = pin.shape[0]
    half = rank // cols
    pack = LANES // rank
    groups = half // pack // PARTS
    piece = SLOTS * groups
    depth = groups * LANES
    width = q_part.shape[1]

    def load(src, dst, sem):
        pltpu.make_async_copy(src, dst, load_sem.at[sem]).start()

    stages = []
    for x, w, v, count in ((act, pin, xl, LEFT_CHUNKS), (grad, pout, xr, RIGHT_CHUNKS)):
        step = x.shape[1] // count
        for i in range(count):
            span = pl.ds(i * step, step)
            load(x.at[:, span], v.at[pl.ds(0, tokens), span], len(stages))
            load(w.at[:, span], v.at[pl.ds(tokens, rank), span], len(stages))
            stages.append(v.at[:, span])
    ids_sem, inv_sem, store_sem = (len(stages) + i for i in range(3))
    load(ids, ids_all.at[me], ids_sem)
    load(inv, inv_v, inv_sem)
    load(store, store_v, store_sem)

    barrier = pltpu.get_barrier_semaphore()
    ctx_peers = {r: {"ctx": jnp.bitwise_xor(me, r)} for r in sends_order(n)}
    peers = [
        {"ctx": jnp.bitwise_xor(me, r), "col": jnp.bitwise_xor(core, d)}
        for r in sends_order(n) + [0]
        for d in range(cols)
        if r or d
    ]
    for peer in peers:
        pl.semaphore_signal(barrier, inc=1, device_id=peer, device_id_type=MESH)

    def send(src, dst, at, peer, to=None):
        pltpu.make_async_remote_copy(
            src_ref=src, dst_ref=dst, send_sem=send_sem.at[at], recv_sem=recv_sem.at[at if to is None else to],
            device_id=peer, device_id_type=MESH,
        ).start()

    totals = []
    for first, count in ((0, LEFT_CHUNKS), (LEFT_CHUNKS, RIGHT_CHUNKS)):
        total = None
        for i in range(first, first + count):
            await_bytes(stages[i], load_sem.at[i])
            v = stages[i]
            term = dot_nt(v[tokens:, :], v[:tokens, :])
            total = term if total is None else total + term
        totals.append(total)
    left, right = totals
    part[:half] = left[:half]
    part[half : half + rank] = right
    part[half + rank :] = left[half:]
    pl.semaphore_wait(barrier, len(peers))
    partner = {"col": other}
    span = pl.ds(pl.multiple_of(other * half, half), half + rank)
    send(part.at[span], came.at[span], 0, partner)
    await_bytes(ids_all.at[me], load_sem.at[ids_sem])
    for peer in ctx_peers.values():
        send(ids, ids_all.at[me], 1, peer)
    own_ids = ids_all[me]
    first = own_ids[:, 0:1]
    masks = [(own_ids == first + s).astype(jnp.float32) for s in range(SLOTS)]
    await_bytes(part.at[pl.ds(0, half + rank)], recv_sem.at[0])
    rows = pl.ds(pl.multiple_of(core * (half + rank), half), half)
    full_l[...] = part[rows, :] + came[rows, :]
    highs, lows = [], []
    for p in range(pack):
        lines = full_l[pl.ds(p, PARTS * groups, stride=pack), :]
        high, low = halves(
            jnp.concatenate(
                [lines[c * groups : (c + 1) * groups] * mask for c in range(PARTS) for mask in masks], axis=0
            )
        )
        highs.append(high)
        lows.append(low)
    weights = jnp.concatenate(highs + highs + lows, axis=1).astype(jnp.bfloat16)
    high, low = halves(part[half : half + rank] + came[half : half + rank])
    zero = jnp.zeros_like(high)

    def diagonal(block, p):
        return [block if q == p else zero for q in range(pack)]

    spread = jnp.concatenate(
        [
            jnp.concatenate(diagonal(high, p) + diagonal(low, p) + diagonal(high, p), axis=1)
            for p in range(pack)
        ],
        axis=0,
    ).astype(jnp.bfloat16)
    product = dot_nt(weights, spread)
    mine = pl.ds(pl.multiple_of(me * piece, 8), piece)
    for c in range(PARTS):
        sums[c, mine, :] = product[c * piece : (c + 1) * piece]
    for c in range(PARTS):
        for peer in ctx_peers.values():
            send(sums.at[c, mine], sums.at[c, mine], 2, peer, 4 + c)

    await_bytes(inv_v, load_sem.at[inv_sem])
    band = LANES

    def split(i, carry):
        rows = pl.ds(pl.multiple_of(i * band, band), band)
        high, low = halves(inv_v[rows, :])
        inv_hi[rows, :] = high.astype(jnp.bfloat16)
        inv_lo[rows, :] = low.astype(jnp.bfloat16)
        return carry

    lax.fori_loop(0, inv_v.shape[0] // band, split, 0)
    await_bytes(store_v, load_sem.at[store_sem])
    store_t[...] = store_v[...].T

    await_bytes(ids_all.at[pl.ds(0, n - 1)], recv_sem.at[1])
    doc_rows = q_part.shape[0]
    column = lax.broadcasted_iota(jnp.int32, (1, SLOTS * n), 1)
    doc_of = jnp.zeros((1, SLOTS * n), jnp.int32)
    for b in range(n):
        inside = (column >= b * SLOTS) & (column < (b + 1) * SLOTS)
        doc_of = jnp.where(inside, ids_all[b][:, 0:1] + (column - b * SLOTS), doc_of)
    pick = (lax.broadcasted_iota(jnp.int32, (doc_rows, SLOTS * n), 0) == doc_of).astype(jnp.float32)

    def take(c):
        await_bytes(sums.at[c, pl.ds(0, (n - 1) * piece)], recv_sem.at[4 + c])
        gathered = jnp.concatenate(
            [sums[c, pl.ds(k, SLOTS * n, stride=groups), :] for k in range(groups)], axis=1
        )
        high, low = halves(gathered)
        return jnp.concatenate([high, low], axis=0).astype(jnp.bfloat16), high.astype(jnp.bfloat16)

    def times(c, side, both, high):
        at = pl.ds(c * depth, depth), pl.ds(pl.multiple_of(side * width, width), width)
        main = dot(both, inv_hi[at])
        return main[: SLOTS * n] + main[SLOTS * n :] + dot(high, inv_lo[at])

    def picked(rows):
        return jnp.dot(pick, rows, precision=lax.Precision.HIGHEST, preferred_element_type=jnp.float32)

    theirs, own = 0.0, 0.0
    for c in range(PARTS):
        taken = take(c)
        theirs = theirs + times(c, other, *taken)
        if c < PARTS - 1:
            own = own + times(c, core, *taken)
    q_part[...] = picked(theirs)
    send(q_part, q_from, 3, partner)
    mine = picked(own + times(PARTS - 1, core, *taken))
    await_bytes(q_part, recv_sem.at[3])
    slot = me * cols + core
    q_all[slot] = (mine + q_from[...]).astype(jnp.bfloat16)
    for peer in peers:
        send(q_all.at[slot], q_all.at[slot], 4, peer, 4 + PARTS)
    await_bytes(q_all.at[pl.ds(0, n * cols - 1)], recv_sem.at[4 + PARTS])
    precond = jnp.concatenate([q_all[i] for i in range(n * cols)], axis=1)
    out[...] = dot(precond, store_t[...])[:docs]
    await_bytes(part.at[pl.ds(0, half + rank)], send_sem.at[0])
    await_bytes(ids_all.at[pl.ds(0, n - 1)], send_sem.at[1])
    await_bytes(sums.at[:, pl.ds(0, (n - 1) * piece)], send_sem.at[2])
    await_bytes(q_part, send_sem.at[3])
    await_bytes(q_all.at[pl.ds(0, n * cols - 1)], send_sem.at[4])


def sends_order(n):
    near = [r for r in range(1, n // 2 + 1)]
    return [s for r in near for s in ((n - r, r) if n - r != r else (r,))]


def fused(n, cols, activations, gradients, doc_ids, proj_in, proj_out, inverse, store_rows):
    tokens = activations.shape[0]
    rank = proj_in.shape[1]
    half = rank // cols
    docs = SLOTS * n // 2
    doc_rows = -(-docs // 16) * 16
    width = inverse.shape[1] // cols
    piece = SLOTS * half * rank // LANES // PARTS
    anywhere = pl.BlockSpec(memory_space=pl.ANY)
    dma = pltpu.SemaphoreType.DMA
    return pl.pallas_call(
        functools.partial(score_kernel, n, cols, docs),
        name="scores",
        out_shape=pltpu.VMEM((docs, store_rows.shape[0]), jnp.float32),
        in_specs=[anywhere] * 7,
        out_specs=pl.BlockSpec(memory_space=pltpu.VMEM),
        scratch_shapes=[
            pltpu.VMEM((tokens + rank, activations.shape[1]), jnp.bfloat16),
            pltpu.VMEM((tokens + rank, gradients.shape[1]), jnp.bfloat16),
            pltpu.VMEM(inverse.shape, jnp.float32),
            pltpu.VMEM(store_rows.shape, jnp.bfloat16),
            pltpu.VMEM(inverse.shape, jnp.bfloat16),
            pltpu.VMEM(inverse.shape, jnp.bfloat16),
            pltpu.VMEM(store_rows.shape[::-1], jnp.bfloat16),
            pltpu.VMEM((n, 1, tokens), jnp.int32),
            pltpu.VMEM((2 * half + rank, tokens), jnp.float32),
            pltpu.VMEM((2 * half + rank, tokens), jnp.float32),
            pltpu.VMEM((half, tokens), jnp.float32),
            pltpu.VMEM((PARTS, n * piece, LANES), jnp.float32),
            pltpu.VMEM((doc_rows, width), jnp.float32),
            pltpu.VMEM((doc_rows, width), jnp.float32),
            pltpu.VMEM((n * cols, doc_rows, width), jnp.bfloat16),
            dma((LEFT_CHUNKS + RIGHT_CHUNKS + 3,)),
            dma((5,)),
            dma((5 + PARTS,)),
        ],
        compiler_params=pltpu.CompilerParams(
            collective_id=0, has_side_effects=True, vmem_limit_bytes=60 << 20
        ),
    )(activations, gradients, doc_ids[None, :], proj_in.T, proj_out.T, inverse, store_rows)


def suits_kernel(n, cols, activations, gradients, proj_in, inverse):
    rank = proj_in.shape[1]
    return (
        cols == 2
        and activations.shape[0] == LANES
        and LANES % rank == 0
        and (rank // cols * rank) % (8 * PARTS * LANES) == 0
        and activations.shape[1] % (LEFT_CHUNKS * LANES) == 0
        and gradients.shape[1] % (RIGHT_CHUNKS * LANES) == 0
        and inverse.shape[1] % (cols * LANES) == 0
        and n <= 16
        and n & (n - 1) == 0
    )


def solution(mesh):
    in_specs = (
        P(("groups", "ctx"), "col"),
        P(("groups", "ctx"), "col"),
        P(("groups", "ctx")),
        P("col", None),
        P("col", None),
        P("col", "ctx"),
        P(("groups", "ctx", "col"), None),
    )
    out_specs = P(None, ("groups", "ctx", "col"))
    n, cols = mesh.shape["ctx"], mesh.shape["col"]

    def body(activations, gradients, doc_ids, proj_in, proj_out, inverse, store_rows):
        args = (activations, gradients, doc_ids, proj_in, proj_out, inverse, store_rows)
        if suits_kernel(n, cols, activations, gradients, proj_in, inverse):
            return fused(n, cols, *args)
        return shards(*args)

    return jax.shard_map(body, mesh=mesh, in_specs=in_specs, out_specs=out_specs, check_vma=False)
```

time: 22.7 us -> 20.7 us (0.912)
  Pallas kernels: 21.2 us -> 20 us
  local copies, waits for them, and re-layouts: 1.3 us -> 0.6 us
    pallas_call x1, Pallas kernels: 21.2 us -> 20 us  [fused(): pl.pallas_call(functools.partial(score_kernel, n, cols, docs), name='scor...]
    unnamed x1, local copies, waits for them, and re-layouts: 1.3 us -> 0.6 us
where the time goes in v1:
time: 20.7 us; the launch traced here: 20.6 us
  Pallas kernels  20 us (97%)
  local copies, waits for them, and re-layouts  0.6 us (3%)
    pallas_call x1, Pallas kernels, fused(): pl.pallas_call(functools.partial(score_kernel, n, cols, docs), name='scor...  20 us
    unnamed x1, local copies, waits for them, and re-layouts  0.6 us

profile of v1, /device:TPU:0, one launch (start us, length us, event | category | flops | bytes accessed | tf_op | source)
XLA Modules:
  0.0 20.6 jit_solution(711023529612680845)
XLA Ops:
  0.0 20.0 %scores.1 = f32[12,64]{1,0:T(8,128)S(1)} custom-call(bf16[128,2048]{1,0:T(8,128)(2,1)} %act.1, bf16[128,7168]{1,0:T(8,128)(2,1)} %grad.1, s32[1,128]{1,0:T(1,128)} %bitcast.5, bf16[64,2048]{1,0:T(8,128)(2,1)} %bitcast.4, bf16[64,7168]{1,0:T(8,128)(2,1)} %bitcast.3, f32[2048,512]{1,0:T(8,128)} %inv.1, bf16[64,4096]{1,0:T(8,128)(2,1)} %store.1), custom_call_target="tpu_custom_call" | custom-call | tf_op jit(solution)/shard_map/scores/pallas_call | solution.py:277
  20.0 0.6 %copy.9 = f32[12,64]{1,0:T(8,128)} copy(f32[12,64]{1,0:T(8,128)S(1)} %scores.1) | data formatting | bytes 6144

commit v2 on v1

--- a/solution.py
+++ b/solution.py
@@ -61,10 +61,10 @@
 
 
 LANES = 128
+ROWS = 8
 SLOTS = 3
 LEFT_CHUNKS = 1
 RIGHT_CHUNKS = 4
-PARTS = 1
 MESH = pl.DeviceIdType.MESH
 NT = (((1,), (1,)), ((), ()))
 
@@ -89,9 +89,9 @@
 def score_kernel(
     n, cols, docs,
     act, grad, ids, pin, pout, inv, store, out,
-    xl, xr, inv_v, store_v, inv_hi, inv_lo, store_t, ids_all,
-    part, came, full_l, sums, q_part, q_from, q_all,
-    load_sem, send_sem, recv_sem,
+    xl, xr, inv_v, store_v, inv_hi, inv_lo, store_t, ids_v,
+    part, came, full_l, notes, sums, q_part, q_from, q_all,
+    load_sem, send_sem, recv_sem, ready,
 ):
     me = lax.axis_index("ctx")
     core = lax.axis_index("col")
@@ -100,10 +100,10 @@
     rank = pin.shape[0]
     half = rank // cols
     pack = LANES // rank
-    groups = half // pack // PARTS
+    groups = half // pack
     piece = SLOTS * groups
-    depth = groups * LANES
     width = q_part.shape[1]
+    spans = width // LANES
 
     def load(src, dst, sem):
         pltpu.make_async_copy(src, dst, load_sem.at[sem]).start()
@@ -117,24 +117,30 @@
             load(w.at[:, span], v.at[pl.ds(tokens, rank), span], len(stages))
             stages.append(v.at[:, span])
     ids_sem, inv_sem, store_sem = (len(stages) + i for i in range(3))
-    load(ids, ids_all.at[me], ids_sem)
+    load(ids, ids_v, ids_sem)
     load(inv, inv_v, inv_sem)
     load(store, store_v, store_sem)
 
     barrier = pltpu.get_barrier_semaphore()
-    ctx_peers = {r: {"ctx": jnp.bitwise_xor(me, r)} for r in sends_order(n)}
-    peers = [
-        {"ctx": jnp.bitwise_xor(me, r), "col": jnp.bitwise_xor(core, d)}
-        for r in sends_order(n) + [0]
-        for d in range(cols)
-        if r or d
-    ]
-    for peer in peers:
-        pl.semaphore_signal(barrier, inc=1, device_id=peer, device_id_type=MESH)
-
-    def send(src, dst, at, peer, to=None):
+    ctx_peers = [{"ctx": there} for there in far_first(me, n)]
+    peers = [peer | {"col": to} for peer in ctx_peers for to in (core, other)]
+    partner = {"col": other}
+
+    @pl.when(core == cols - 1)
+    def _():
+        pl.semaphore_signal(barrier, inc=1, device_id=partner, device_id_type=MESH)
+
+    for peer in ctx_peers:
+        pl.semaphore_signal(barrier, inc=1, device_id=peer | {"col": cols - 1}, device_id_type=MESH)
+
+    @pl.when(core == 0)
+    def _():
+        pl.semaphore_wait(barrier, 1)
+        pl.semaphore_signal(ready, inc=1, device_id=partner, device_id_type=MESH)
+
+    def send(src, dst, at, peer):
         pltpu.make_async_remote_copy(
-            src_ref=src, dst_ref=dst, send_sem=send_sem.at[at], recv_sem=recv_sem.at[at if to is None else to],
+            src_ref=src, dst_ref=dst, send_sem=send_sem.at[at], recv_sem=recv_sem.at[at],
             device_id=peer, device_id_type=MESH,
         ).start()
 
@@ -151,14 +157,20 @@
     part[:half] = left[:half]
     part[half : half + rank] = right
     part[half + rank :] = left[half:]
-    pl.semaphore_wait(barrier, len(peers))
-    partner = {"col": other}
+    @pl.when(core == cols - 1)
+    def _():
+        pl.semaphore_wait(ready, 1)
+
     span = pl.ds(pl.multiple_of(other * half, half), half + rank)
     send(part.at[span], came.at[span], 0, partner)
-    await_bytes(ids_all.at[me], load_sem.at[ids_sem])
-    for peer in ctx_peers.values():
-        send(ids, ids_all.at[me], 1, peer)
-    own_ids = ids_all[me]
+
+    @pl.when(core == cols - 1)
+    def _():
+        pl.semaphore_wait(barrier, cols * (n - 1))
+        pl.semaphore_signal(ready, inc=1, device_id=partner, device_id_type=MESH)
+
+    await_bytes(ids_v, load_sem.at[ids_sem])
+    own_ids = ids_v[...]
     first = own_ids[:, 0:1]
     masks = [(own_ids == first + s).astype(jnp.float32) for s in range(SLOTS)]
     await_bytes(part.at[pl.ds(0, half + rank)], recv_sem.at[0])
@@ -166,12 +178,8 @@
     full_l[...] = part[rows, :] + came[rows, :]
     highs, lows = [], []
     for p in range(pack):
-        lines = full_l[pl.ds(p, PARTS * groups, stride=pack), :]
-        high, low = halves(
-            jnp.concatenate(
-                [lines[c * groups : (c + 1) * groups] * mask for c in range(PARTS) for mask in masks], axis=0
-            )
-        )
+        lines = full_l[pl.ds(p, groups, stride=pack), :]
+        high, low = halves(jnp.concatenate([lines * mask for mask in masks], axis=0))
         highs.append(high)
         lows.append(low)
     weights = jnp.concatenate(highs + highs + lows, axis=1).astype(jnp.bfloat16)
@@ -188,13 +196,17 @@
         ],
         axis=0,
     ).astype(jnp.bfloat16)
-    product = dot_nt(weights, spread)
-    mine = pl.ds(pl.multiple_of(me * piece, 8), piece)
-    for c in range(PARTS):
-        sums[c, mine, :] = product[c * piece : (c + 1) * piece]
-    for c in range(PARTS):
-        for peer in ctx_peers.values():
-            send(sums.at[c, mine], sums.at[c, mine], 2, peer, 4 + c)
+    mine = pl.ds(pl.multiple_of(me * piece, ROWS), piece)
+    notes[me] = jnp.broadcast_to(first, (1, LANES)).astype(jnp.float32)
+    sums[mine, :] = dot_nt(weights, spread)
+
+    @pl.when(core == 0)
+    def _():
+        pl.semaphore_wait(ready, 1)
+
+    for peer in ctx_peers:
+        send(notes.at[me], notes.at[me], 4, peer)
+        send(sums.at[mine], sums.at[mine], 1, peer)
 
     await_bytes(inv_v, load_sem.at[inv_sem])
     band = LANES
@@ -208,60 +220,74 @@
 
     lax.fori_loop(0, inv_v.shape[0] // band, split, 0)
     await_bytes(store_v, load_sem.at[store_sem])
-    store_t[...] = store_v[...].T
-
-    await_bytes(ids_all.at[pl.ds(0, n - 1)], recv_sem.at[1])
+    stored = store_v.shape[0]
+    for i in range(n * cols):
+        tiles = []
+        for j in range(spans):
+            tile = (i * spans + j) * LANES
+            tiles.append(store_v[:, tile : tile + LANES])
+        store_t[i * LANES : (i + 1) * LANES, :] = jnp.concatenate(tiles, axis=0).T
+
+    await_bytes(notes.at[pl.ds(0, n - 1)], recv_sem.at[4])
+    await_bytes(sums.at[pl.ds(0, (n - 1) * piece)], recv_sem.at[1])
+    gathered = jnp.concatenate(
+        [sums[pl.ds(k, SLOTS * n, stride=groups), :] for k in range(groups)], axis=1
+    )
+    high, low = halves(gathered)
+    both = jnp.concatenate([high, low], axis=0).astype(jnp.bfloat16)
+    high = high.astype(jnp.bfloat16)
     doc_rows = q_part.shape[0]
     column = lax.broadcasted_iota(jnp.int32, (1, SLOTS * n), 1)
-    doc_of = jnp.zeros((1, SLOTS * n), jnp.int32)
+    doc_of = jnp.zeros((1, SLOTS * n), jnp.float32)
     for b in range(n):
-        inside = (column >= b * SLOTS) & (column < (b + 1) * SLOTS)
-        doc_of = jnp.where(inside, ids_all[b][:, 0:1] + (column - b * SLOTS), doc_of)
-    pick = (lax.broadcasted_iota(jnp.int32, (doc_rows, SLOTS * n), 0) == doc_of).astype(jnp.float32)
-
-    def take(c):
-        await_bytes(sums.at[c, pl.ds(0, (n - 1) * piece)], recv_sem.at[4 + c])
-        gathered = jnp.concatenate(
-            [sums[c, pl.ds(k, SLOTS * n, stride=groups), :] for k in range(groups)], axis=1
-        )
-        high, low = halves(gathered)
-        return jnp.concatenate([high, low], axis=0).astype(jnp.bfloat16), high.astype(jnp.bfloat16)
-
-    def times(c, side, both, high):
-        at = pl.ds(c * depth, depth), pl.ds(pl.multiple_of(side * width, width), width)
-        main = dot(both, inv_hi[at])
-        return main[: SLOTS * n] + main[SLOTS * n :] + dot(high, inv_lo[at])
-
-    def picked(rows):
-        return jnp.dot(pick, rows, precision=lax.Precision.HIGHEST, preferred_element_type=jnp.float32)
-
-    theirs, own = 0.0, 0.0
-    for c in range(PARTS):
-        taken = take(c)
-        theirs = theirs + times(c, other, *taken)
-        if c < PARTS - 1:
-            own = own + times(c, core, *taken)
-    q_part[...] = picked(theirs)
-    send(q_part, q_from, 3, partner)
-    mine = picked(own + times(PARTS - 1, core, *taken))
-    await_bytes(q_part, recv_sem.at[3])
+        for s in range(SLOTS):
+            doc_of = jnp.where(column == b * SLOTS + s, notes[b][:, :1] + s, doc_of)
+    docs_at = lax.broadcasted_iota(jnp.int32, (doc_rows, SLOTS * n), 0).astype(jnp.float32)
+    pick = (docs_at == doc_of).astype(jnp.bfloat16)
+    pick = jnp.concatenate([pick, pick, pick], axis=1)
+
+    def picked(side):
+        at = pl.ds(pl.multiple_of(side * width, width), width)
+        main = dot(both, inv_hi[:, at])
+        rows = main[: SLOTS * n] + main[SLOTS * n :] + dot(high, inv_lo[:, at])
+        high_rows, rest = halves(rows)
+        middle, low_rows = halves(rest)
+        return dot(pick, jnp.concatenate([high_rows, middle, low_rows], axis=0).astype(jnp.bfloat16))
+
+    q_part[...] = picked(other)
+    send(q_part, q_from, 2, partner)
+    own = picked(core)
+    await_bytes(q_part, recv_sem.at[2])
     slot = me * cols + core
-    q_all[slot] = (mine + q_from[...]).astype(jnp.bfloat16)
-    for peer in peers:
-        send(q_all.at[slot], q_all.at[slot], 4, peer, 4 + PARTS)
-    await_bytes(q_all.at[pl.ds(0, n * cols - 1)], recv_sem.at[4 + PARTS])
+    total = own + q_from[...]
+    q_all[slot] = jnp.concatenate(
+        [total[:docs, j * LANES : (j + 1) * LANES] for j in range(spans)], axis=0
+    ).astype(jnp.bfloat16)
+    for peer in peers + [partner]:
+        send(q_all.at[slot], q_all.at[slot], 3, peer)
+    await_bytes(q_all.at[pl.ds(0, n * cols - 1)], recv_sem.at[3])
     precond = jnp.concatenate([q_all[i] for i in range(n * cols)], axis=1)
-    out[...] = dot(precond, store_t[...])[:docs]
+    scores = dot(precond, store_t[...])
+    out[...] = sum(scores[j * docs : (j + 1) * docs, j * stored : (j + 1) * stored] for j in range(spans))
     await_bytes(part.at[pl.ds(0, half + rank)], send_sem.at[0])
-    await_bytes(ids_all.at[pl.ds(0, n - 1)], send_sem.at[1])
-    await_bytes(sums.at[:, pl.ds(0, (n - 1) * piece)], send_sem.at[2])
-    await_bytes(q_part, send_sem.at[3])
-    await_bytes(q_all.at[pl.ds(0, n * cols - 1)], send_sem.at[4])
-
-
-def sends_order(n):
-    near = [r for r in range(1, n // 2 + 1)]
-    return [s for r in near for s in ((n - r, r) if n - r != r else (r,))]
+    await_bytes(sums.at[pl.ds(0, (n - 1) * piece)], send_sem.at[1])
+    await_bytes(notes.at[pl.ds(0, n - 1)], send_sem.at[4])
+    await_bytes(q_part, send_sem.at[2])
+    await_bytes(q_all.at[pl.ds(0, n * cols - 1)], send_sem.at[3])
+
+
+def far_first(me, n):
+    rows = n // 2
+    row, side = me // 2, me % 2
+    upper = row >= rows // 2
+    near = jnp.where(upper, rows - 1 - row, row)
+    order = []
+    for j in range(rows - 1):
+        there = rows - 1 - j
+        there = there - (there <= near).astype(jnp.int32)
+        there = jnp.where(upper, rows - 1 - there, there)
+        order += [2 * there + 1 - side, 2 * there + side]
+    return order + [2 * row + 1 - side]
 
 
 def fused(n, cols, activations, gradients, doc_ids, proj_in, proj_out, inverse, store_rows):
@@ -271,7 +297,8 @@
     docs = SLOTS * n // 2
     doc_rows = -(-docs // 16) * 16
     width = inverse.shape[1] // cols
-    piece = SLOTS * half * rank // LANES // PARTS
+    spans = width // LANES
+    piece = SLOTS * half * rank // LANES
     anywhere = pl.BlockSpec(memory_space=pl.ANY)
     dma = pltpu.SemaphoreType.DMA
     return pl.pallas_call(
@@ -287,18 +314,20 @@
             pltpu.VMEM(store_rows.shape, jnp.bfloat16),
             pltpu.VMEM(inverse.shape, jnp.bfloat16),
             pltpu.VMEM(inverse.shape, jnp.bfloat16),
-            pltpu.VMEM(store_rows.shape[::-1], jnp.bfloat16),
-            pltpu.VMEM((n, 1, tokens), jnp.int32),
+            pltpu.VMEM((store_rows.shape[1] // spans, spans * store_rows.shape[0]), jnp.bfloat16),
+            pltpu.VMEM((1, tokens), jnp.int32),
             pltpu.VMEM((2 * half + rank, tokens), jnp.float32),
             pltpu.VMEM((2 * half + rank, tokens), jnp.float32),
             pltpu.VMEM((half, tokens), jnp.float32),
-            pltpu.VMEM((PARTS, n * piece, LANES), jnp.float32),
+            pltpu.VMEM((n, 1, LANES), jnp.float32),
+            pltpu.VMEM((n * piece, LANES), jnp.float32),
             pltpu.VMEM((doc_rows, width), jnp.float32),
             pltpu.VMEM((doc_rows, width), jnp.float32),
-            pltpu.VMEM((n * cols, doc_rows, width), jnp.bfloat16),
+            pltpu.VMEM((n * cols, spans * docs, LANES), jnp.bfloat16),
             dma((LEFT_CHUNKS + RIGHT_CHUNKS + 3,)),
             dma((5,)),
-            dma((5 + PARTS,)),
+            dma((5,)),
+            pltpu.SemaphoreType.REGULAR,
         ],
         compiler_params=pltpu.CompilerParams(
             collective_id=0, has_side_effects=True, vmem_limit_bytes=60 << 20
@@ -312,11 +341,11 @@
         cols == 2
         and activations.shape[0] == LANES
         and LANES % rank == 0
-        and (rank // cols * rank) % (8 * PARTS * LANES) == 0
+        and (rank // cols * rank) % (ROWS * LANES) == 0
         and activations.shape[1] % (LEFT_CHUNKS * LANES) == 0
         and gradients.shape[1] % (RIGHT_CHUNKS * LANES) == 0
         and inverse.shape[1] % (cols * LANES) == 0
-        and n <= 16
+        and 8 <= n <= 16
         and n & (n - 1) == 0
     )
 

time: 20.7 us -> 19.8 us (0.957)
  Pallas kernels: 20 us -> 19.1 us
    pallas_call x1, Pallas kernels: 20 us -> 19.1 us  [fused(): pl.pallas_call(functools.partial(score_kernel, n, cols, docs), name='scor...]
where the time goes in v2:
time: 19.8 us; the launch traced here: 19.7 us
  Pallas kernels  19.1 us (96%)
  local copies, waits for them, and re-layouts  0.6 us (3%)
    pallas_call x1, Pallas kernels, fused(): pl.pallas_call(functools.partial(score_kernel, n, cols, docs), name='scor...  19.1 us
    unnamed x1, local copies, waits for them, and re-layouts  0.6 us

profile of v2, /device:TPU:0, one launch (start us, length us, event | category | flops | bytes accessed | tf_op | source)
XLA Modules:
  0.0 19.7 jit_solution(17740624454621472140)
XLA Ops:
  0.0 19.1 %scores.1 = f32[12,64]{1,0:T(8,128)S(1)} custom-call(bf16[128,2048]{1,0:T(8,128)(2,1)} %act.1, bf16[128,7168]{1,0:T(8,128)(2,1)} %grad.1, s32[1,128]{1,0:T(1,128)} %bitcast.5, bf16[64,2048]{1,0:T(8,128)(2,1)} %bitcast.4, bf16[64,7168]{1,0:T(8,128)(2,1)} %bitcast.3, f32[2048,512]{1,0:T(8,128)} %inv.1, bf16[64,4096]{1,0:T(8,128)(2,1)} %store.1), custom_call_target="tpu_custom_call" | custom-call | tf_op jit(solution)/shard_map/scores/pallas_call | solution.py:304
  19.1 0.6 %copy.9 = f32[12,64]{1,0:T(8,128)} copy(f32[12,64]{1,0:T(8,128)S(1)} %scores.1) | data formatting | bytes 6144

commit v3 on v2

--- a/solution.py
+++ b/solution.py
@@ -63,6 +63,8 @@
 LANES = 128
 ROWS = 8
 SLOTS = 3
+STEPS = 32767.0
+LEAST = 2.0**-110
 LEFT_CHUNKS = 1
 RIGHT_CHUNKS = 4
 MESH = pl.DeviceIdType.MESH
@@ -90,7 +92,7 @@
     n, cols, docs,
     act, grad, ids, pin, pout, inv, store, out,
     xl, xr, inv_v, store_v, inv_hi, inv_lo, store_t, ids_v,
-    part, came, full_l, notes, sums, q_part, q_from, q_all,
+    part, came, full_l, codes, notes, sums, q_part, q_from, q_all,
     load_sem, send_sem, recv_sem, ready,
 ):
     me = lax.axis_index("ctx")
@@ -196,9 +198,19 @@
         ],
         axis=0,
     ).astype(jnp.bfloat16)
-    mine = pl.ds(pl.multiple_of(me * piece, ROWS), piece)
-    notes[me] = jnp.broadcast_to(first, (1, LANES)).astype(jnp.float32)
-    sums[mine, :] = dot_nt(weights, spread)
+    mine = pl.ds(pl.multiple_of(me * piece, 2 * ROWS), piece)
+    product = dot_nt(weights, spread)
+    lane = lax.broadcasted_iota(jnp.int32, (1, LANES), 1)
+    note = jnp.broadcast_to(first.astype(jnp.float32), (1, LANES))
+    coded = []
+    for s in range(SLOTS):
+        rows_s = product[s * groups : (s + 1) * groups]
+        top = jnp.max(jnp.max(jnp.abs(rows_s), axis=0, keepdims=True), axis=1, keepdims=True)
+        top = jnp.maximum(top, LEAST)
+        coded.append(jnp.floor(rows_s * (STEPS / top) + 0.5))
+        note = jnp.where(lane > s, top * (1.0 / STEPS), note)
+    notes[me] = note
+    codes[mine, :] = jnp.concatenate(coded, axis=0).astype(jnp.int32).astype(jnp.int16)
 
     @pl.when(core == 0)
     def _():
@@ -206,7 +218,7 @@
 
     for peer in ctx_peers:
         send(notes.at[me], notes.at[me], 4, peer)
-        send(sums.at[mine], sums.at[mine], 1, peer)
+        send(codes.at[mine], codes.at[mine], 1, peer)
 
     await_bytes(inv_v, load_sem.at[inv_sem])
     band = LANES
@@ -229,7 +241,11 @@
         store_t[i * LANES : (i + 1) * LANES, :] = jnp.concatenate(tiles, axis=0).T
 
     await_bytes(notes.at[pl.ds(0, n - 1)], recv_sem.at[4])
-    await_bytes(sums.at[pl.ds(0, (n - 1) * piece)], recv_sem.at[1])
+    await_bytes(codes.at[pl.ds(0, (n - 1) * piece)], recv_sem.at[1])
+    for b in range(n):
+        for s in range(SLOTS):
+            at = slice(b * piece + s * groups, b * piece + (s + 1) * groups)
+            sums[at] = codes[at].astype(jnp.int32).astype(jnp.float32) * notes[b][:, s + 1 : s + 2]
     gathered = jnp.concatenate(
         [sums[pl.ds(k, SLOTS * n, stride=groups), :] for k in range(groups)], axis=1
     )
@@ -270,7 +286,7 @@
     scores = dot(precond, store_t[...])
     out[...] = sum(scores[j * docs : (j + 1) * docs, j * stored : (j + 1) * stored] for j in range(spans))
     await_bytes(part.at[pl.ds(0, half + rank)], send_sem.at[0])
-    await_bytes(sums.at[pl.ds(0, (n - 1) * piece)], send_sem.at[1])
+    await_bytes(codes.at[pl.ds(0, (n - 1) * piece)], send_sem.at[1])
     await_bytes(notes.at[pl.ds(0, n - 1)], send_sem.at[4])
     await_bytes(q_part, send_sem.at[2])
     await_bytes(q_all.at[pl.ds(0, n * cols - 1)], send_sem.at[3])
@@ -319,6 +335,7 @@
             pltpu.VMEM((2 * half + rank, tokens), jnp.float32),
             pltpu.VMEM((2 * half + rank, tokens), jnp.float32),
             pltpu.VMEM((half, tokens), jnp.float32),
+            pltpu.VMEM((n * piece, LANES), jnp.int16),
             pltpu.VMEM((n, 1, LANES), jnp.float32),
             pltpu.VMEM((n * piece, LANES), jnp.float32),
             pltpu.VMEM((doc_rows, width), jnp.float32),

time: 19.8 us -> 18.5 us (0.934)
  Pallas kernels: 19.1 us -> 17.7 us
    pallas_call x1, Pallas kernels: 19.1 us -> 17.7 us  [fused(): pl.pallas_call(functools.partial(score_kernel, n, cols, docs), name='scor...]
where the time goes in v3:
time: 18.5 us; the launch traced here: 18.3 us
  Pallas kernels  17.7 us (96%)
  local copies, waits for them, and re-layouts  0.6 us (3%)
    pallas_call x1, Pallas kernels, fused(): pl.pallas_call(functools.partial(score_kernel, n, cols, docs), name='scor...  17.7 us
    unnamed x1, local copies, waits for them, and re-layouts  0.6 us

profile of v3, /device:TPU:0, one launch (start us, length us, event | category | flops | bytes accessed | tf_op | source)
XLA Modules:
  0.0 18.3 jit_solution(11582256413596681168)
XLA Ops:
  0.0 17.7 %scores.1 = f32[12,64]{1,0:T(8,128)S(1)} custom-call(bf16[128,2048]{1,0:T(8,128)(2,1)} %act.1, bf16[128,7168]{1,0:T(8,128)(2,1)} %grad.1, s32[1,128]{1,0:T(1,128)} %bitcast.5, bf16[64,2048]{1,0:T(8,128)(2,1)} %bitcast.4, bf16[64,7168]{1,0:T(8,128)(2,1)} %bitcast.3, f32[2048,512]{1,0:T(8,128)} %inv.1, bf16[64,4096]{1,0:T(8,128)(2,1)} %store.1), custom_call_target="tpu_custom_call" | custom-call | tf_op jit(solution)/shard_map/scores/pallas_call | solution.py:320
  17.7 0.6 %copy.9 = f32[12,64]{1,0:T(8,128)} copy(f32[12,64]{1,0:T(8,128)S(1)} %scores.1) | data formatting | bytes 6144

commit v4 on v3

--- a/solution.py
+++ b/solution.py
@@ -92,14 +92,14 @@
     n, cols, docs,
     act, grad, ids, pin, pout, inv, store, out,
     xl, xr, inv_v, store_v, inv_hi, inv_lo, store_t, ids_v,
-    part, came, full_l, codes, notes, sums, q_part, q_from, q_all,
+    part, came, full_l, codes, notes, tally, sums, q_part, q_from, q_all,
     load_sem, send_sem, recv_sem, ready,
 ):
     me = lax.axis_index("ctx")
     core = lax.axis_index("col")
     other = cols - 1 - core
-    tokens = act.shape[0]
-    rank = pin.shape[0]
+    tokens = act.shape[0] * ROWS
+    rank = pin.shape[0] * ROWS
     half = rank // cols
     pack = LANES // rank
     groups = half // pack
@@ -107,6 +107,18 @@
     width = q_part.shape[1]
     spans = width // LANES
 
+    barrier = pltpu.get_barrier_semaphore()
+    ctx_peers = [{"ctx": there} for there in far_first(me, n)]
+    peers = [peer | {"col": to} for peer in ctx_peers for to in (core, other)]
+    partner = {"col": other}
+
+    @pl.when(core == cols - 1)
+    def _():
+        pl.semaphore_signal(barrier, inc=1, device_id=partner, device_id_type=MESH)
+
+    for peer in ctx_peers:
+        pl.semaphore_signal(barrier, inc=1, device_id=peer | {"col": cols - 1}, device_id_type=MESH)
+
     def load(src, dst, sem):
         pltpu.make_async_copy(src, dst, load_sem.at[sem]).start()
 
@@ -115,26 +127,15 @@
         step = x.shape[1] // count
         for i in range(count):
             span = pl.ds(i * step, step)
-            load(x.at[:, span], v.at[pl.ds(0, tokens), span], len(stages))
-            load(w.at[:, span], v.at[pl.ds(tokens, rank), span], len(stages))
-            stages.append(v.at[:, span])
+            for source, row in ((x, 0), (w, tokens)):
+                for j in range(source.shape[0]):
+                    load(source.at[j, span], v.at[span, pl.ds(row + j * ROWS, ROWS)], len(stages))
+            stages.append(v.at[span])
     ids_sem, inv_sem, store_sem = (len(stages) + i for i in range(3))
     load(ids, ids_v, ids_sem)
     load(inv, inv_v, inv_sem)
     load(store, store_v, store_sem)
 
-    barrier = pltpu.get_barrier_semaphore()
-    ctx_peers = [{"ctx": there} for there in far_first(me, n)]
-    peers = [peer | {"col": to} for peer in ctx_peers for to in (core, other)]
-    partner = {"col": other}
-
-    @pl.when(core == cols - 1)
-    def _():
-        pl.semaphore_signal(barrier, inc=1, device_id=partner, device_id_type=MESH)
-
-    for peer in ctx_peers:
-        pl.semaphore_signal(barrier, inc=1, device_id=peer | {"col": cols - 1}, device_id_type=MESH)
-
     @pl.when(core == 0)
     def _():
         pl.semaphore_wait(barrier, 1)
@@ -142,7 +143,7 @@
 
     def send(src, dst, at, peer):
         pltpu.make_async_remote_copy(
-            src_ref=src, dst_ref=dst, send_sem=send_sem.at[at], recv_sem=recv_sem.at[at],
+            src_ref=src, dst_ref=dst, send_sem=send_sem.at[0], recv_sem=recv_sem.at[at],
             device_id=peer, device_id_type=MESH,
         ).start()
 
@@ -151,8 +152,15 @@
         total = None
         for i in range(first, first + count):
             await_bytes(stages[i], load_sem.at[i])
-            v = stages[i]
-            term = dot_nt(v[tokens:, :], v[:tokens, :])
+            tiles = stages[i].shape[0]
+            cuts = 2 if i >= LEFT_CHUNKS + RIGHT_CHUNKS - 2 else 1
+            terms = []
+            for c in range(cuts):
+                deep = jnp.concatenate(
+                    [stages[i][k] for k in range(c * tiles // cuts, (c + 1) * tiles // cuts)], axis=1
+                )
+                terms.append(dot_nt(deep[tokens:], deep[:tokens]))
+            term = sum(terms[1:], terms[0])
             total = term if total is None else total + term
         totals.append(total)
     left, right = totals
@@ -217,8 +225,9 @@
         pl.semaphore_wait(ready, 1)
 
     for peer in ctx_peers:
-        send(notes.at[me], notes.at[me], 4, peer)
-        send(codes.at[mine], codes.at[mine], 1, peer)
+        wave = 1 + 3 * (jnp.bitwise_xor(me, peer["ctx"]) // 2 % 2)
+        send(notes.at[me], notes.at[me], wave, peer)
+        send(codes.at[mine], codes.at[mine], wave, peer)
 
     await_bytes(inv_v, load_sem.at[inv_sem])
     band = LANES
@@ -240,14 +249,22 @@
             tiles.append(store_v[:, tile : tile + LANES])
         store_t[i * LANES : (i + 1) * LANES, :] = jnp.concatenate(tiles, axis=0).T
 
-    await_bytes(notes.at[pl.ds(0, n - 1)], recv_sem.at[4])
-    await_bytes(codes.at[pl.ds(0, (n - 1) * piece)], recv_sem.at[1])
-    for b in range(n):
+    def decode(r):
+        there = jnp.bitwise_xor(me, r)
+        note = notes[there]
+        block = codes[pl.ds(pl.multiple_of(there * piece, 2 * ROWS), piece), :].astype(jnp.int32).astype(jnp.float32)
         for s in range(SLOTS):
-            at = slice(b * piece + s * groups, b * piece + (s + 1) * groups)
-            sums[at] = codes[at].astype(jnp.int32).astype(jnp.float32) * notes[b][:, s + 1 : s + 2]
+            rows = block[s * groups : (s + 1) * groups] * note[:, s + 1 : s + 2]
+            sums[pl.ds(r * SLOTS + s, groups, stride=SLOTS * n), :] = rows
+
+    decode(0)
+    for wave, senders in ((4, n // 2), (1, n // 2 - 1)):
+        await_bytes(tally.at[pl.ds(0, senders * (1 + piece // 2))], recv_sem.at[wave])
+        for r in range(1, n):
+            if (r // 2 % 2 == 1) == (wave == 4):
+                decode(r)
     gathered = jnp.concatenate(
-        [sums[pl.ds(k, SLOTS * n, stride=groups), :] for k in range(groups)], axis=1
+        [sums[k * SLOTS * n : (k + 1) * SLOTS * n, :] for k in range(groups)], axis=1
     )
     high, low = halves(gathered)
     both = jnp.concatenate([high, low], axis=0).astype(jnp.bfloat16)
@@ -255,9 +272,9 @@
     doc_rows = q_part.shape[0]
     column = lax.broadcasted_iota(jnp.int32, (1, SLOTS * n), 1)
     doc_of = jnp.zeros((1, SLOTS * n), jnp.float32)
-    for b in range(n):
+    for r in range(n):
         for s in range(SLOTS):
-            doc_of = jnp.where(column == b * SLOTS + s, notes[b][:, :1] + s, doc_of)
+            doc_of = jnp.where(column == r * SLOTS + s, notes[jnp.bitwise_xor(me, r)][:, :1] + s, doc_of)
     docs_at = lax.broadcasted_iota(jnp.int32, (doc_rows, SLOTS * n), 0).astype(jnp.float32)
     pick = (docs_at == doc_of).astype(jnp.bfloat16)
     pick = jnp.concatenate([pick, pick, pick], axis=1)
@@ -285,11 +302,7 @@
     precond = jnp.concatenate([q_all[i] for i in range(n * cols)], axis=1)
     scores = dot(precond, store_t[...])
     out[...] = sum(scores[j * docs : (j + 1) * docs, j * stored : (j + 1) * stored] for j in range(spans))
-    await_bytes(part.at[pl.ds(0, half + rank)], send_sem.at[0])
-    await_bytes(codes.at[pl.ds(0, (n - 1) * piece)], send_sem.at[1])
-    await_bytes(notes.at[pl.ds(0, n - 1)], send_sem.at[4])
-    await_bytes(q_part, send_sem.at[2])
-    await_bytes(q_all.at[pl.ds(0, n * cols - 1)], send_sem.at[3])
+    await_bytes(tally, send_sem.at[0])
 
 
 def far_first(me, n):
@@ -303,7 +316,12 @@
         there = there - (there <= near).astype(jnp.int32)
         there = jnp.where(upper, rows - 1 - there, there)
         order += [2 * there + 1 - side, 2 * there + side]
-    return order + [2 * row + 1 - side]
+    return order[:2] + [2 * row + 1 - side] + order[2:]
+
+
+def tiled(x):
+    rows, columns = x.shape
+    return x.reshape(rows // ROWS, ROWS, columns // LANES, LANES).transpose(0, 2, 1, 3)
 
 
 def fused(n, cols, activations, gradients, doc_ids, proj_in, proj_out, inverse, store_rows):
@@ -315,6 +333,8 @@
     width = inverse.shape[1] // cols
     spans = width // LANES
     piece = SLOTS * half * rank // LANES
+    sent = 4 * (half + rank) * tokens + (n - 1) * (4 + 2 * piece) * LANES + 4 * doc_rows * width
+    sent += (n * cols - 1) * 2 * spans * docs * LANES
     anywhere = pl.BlockSpec(memory_space=pl.ANY)
     dma = pltpu.SemaphoreType.DMA
     return pl.pallas_call(
@@ -324,8 +344,8 @@
         in_specs=[anywhere] * 7,
         out_specs=pl.BlockSpec(memory_space=pltpu.VMEM),
         scratch_shapes=[
-            pltpu.VMEM((tokens + rank, activations.shape[1]), jnp.bfloat16),
-            pltpu.VMEM((tokens + rank, gradients.shape[1]), jnp.bfloat16),
+            pltpu.VMEM((activations.shape[1] // LANES, tokens + rank, LANES), jnp.bfloat16),
+            pltpu.VMEM((gradients.shape[1] // LANES, tokens + rank, LANES), jnp.bfloat16),
             pltpu.VMEM(inverse.shape, jnp.float32),
             pltpu.VMEM(store_rows.shape, jnp.bfloat16),
             pltpu.VMEM(inverse.shape, jnp.bfloat16),
@@ -337,19 +357,20 @@
             pltpu.VMEM((half, tokens), jnp.float32),
             pltpu.VMEM((n * piece, LANES), jnp.int16),
             pltpu.VMEM((n, 1, LANES), jnp.float32),
+            pltpu.VMEM((sent // (4 * LANES), 1, LANES), jnp.float32),
             pltpu.VMEM((n * piece, LANES), jnp.float32),
             pltpu.VMEM((doc_rows, width), jnp.float32),
             pltpu.VMEM((doc_rows, width), jnp.float32),
             pltpu.VMEM((n * cols, spans * docs, LANES), jnp.bfloat16),
             dma((LEFT_CHUNKS + RIGHT_CHUNKS + 3,)),
-            dma((5,)),
+            dma((1,)),
             dma((5,)),
             pltpu.SemaphoreType.REGULAR,
         ],
         compiler_params=pltpu.CompilerParams(
             collective_id=0, has_side_effects=True, vmem_limit_bytes=60 << 20
         ),
-    )(activations, gradients, doc_ids[None, :], proj_in.T, proj_out.T, inverse, store_rows)
+    )(tiled(activations), tiled(gradients), doc_ids[None, :], tiled(proj_in.T), tiled(proj_out.T), inverse, store_rows)
 
 
 def suits_kernel(n, cols, activations, gradients, proj_in, inverse):

time: 18.5 us -> 18.4 us (level)
  no operation moved by 1% of the time
where the time goes in v4:
time: 18.4 us; the launch traced here: 18.3 us
  Pallas kernels  17.7 us (96%)
  local copies, waits for them, and re-layouts  0.6 us (3%)
    pallas_call x1, Pallas kernels, fused(): pl.pallas_call(functools.partial(score_kernel, n, cols, docs), name='scor...  17.7 us
    unnamed x1, local copies, waits for them, and re-layouts  0.6 us

profile of v4, /device:TPU:0, one launch (start us, length us, event | category | flops | bytes accessed | tf_op | source)
XLA Modules:
  0.0 18.3 jit_solution(9748161659344287568)
XLA Ops:
  0.0 17.7 %scores.1 = f32[12,64]{1,0:T(8,128)S(1)} custom-call(bf16[16,16,8,128]{3,2,1,0:T(8,128)(2,1)} %bitcast.19, bf16[16,56,8,128]{3,2,1,0:T(8,128)(2,1)} %bitcast.17, s32[1,128]{1,0:T(1,128)} %bitcast.21, bf16[8,16,8,128]{3,2,1,0:T(8,128)(2,1)} %bitcast.20, bf16[8,56,8,128]{3,2,1,0:T(8,128)(2,1)} %bitcast.18, f32[2048,512]{1,0:T(8,128)} %inv.1, ...), custom_call_target="tpu_custom_call" | custom-call | tf_op jit(solution)/shard_map/scores/pallas_call | solution.py:340
  17.7 0.6 %copy.9 = f32[12,64]{1,0:T(8,128)} copy(f32[12,64]{1,0:T(8,128)S(1)} %scores.1) | data formatting | bytes 6144

commit v5 on v4

--- a/solution.py
+++ b/solution.py
@@ -109,7 +109,7 @@
 
     barrier = pltpu.get_barrier_semaphore()
     ctx_peers = [{"ctx": there} for there in far_first(me, n)]
-    peers = [peer | {"col": to} for peer in ctx_peers for to in (core, other)]
+    peers = [peer | {"col": to} for peer in ctx_peers for to in (0, 1)]
     partner = {"col": other}
 
     @pl.when(core == cols - 1)

time: 18.4 us -> 18.3 us (level)
  no operation moved by 1% of the time
where the time goes in v5:
time: 18.3 us; the launch traced here: 18.2 us
  Pallas kernels  17.6 us (96%)
  local copies, waits for them, and re-layouts  0.6 us (3%)
    pallas_call x1, Pallas kernels, fused(): pl.pallas_call(functools.partial(score_kernel, n, cols, docs), name='scor...  17.6 us
    unnamed x1, local copies, waits for them, and re-layouts  0.6 us

profile of v5, /device:TPU:0, one launch (start us, length us, event | category | flops | bytes accessed | tf_op | source)
XLA Modules:
  0.0 18.2 jit_solution(1949142179225483403)
XLA Ops:
  0.0 17.6 %scores.1 = f32[12,64]{1,0:T(8,128)S(1)} custom-call(bf16[16,16,8,128]{3,2,1,0:T(8,128)(2,1)} %bitcast.19, bf16[16,56,8,128]{3,2,1,0:T(8,128)(2,1)} %bitcast.17, s32[1,128]{1,0:T(1,128)} %bitcast.21, bf16[8,16,8,128]{3,2,1,0:T(8,128)(2,1)} %bitcast.20, bf16[8,56,8,128]{3,2,1,0:T(8,128)(2,1)} %bitcast.18, f32[2048,512]{1,0:T(8,128)} %inv.1, ...), custom_call_target="tpu_custom_call" | custom-call | tf_op jit(solution)/shard_map/scores/pallas_call | solution.py:340
  17.6 0.6 %copy.9 = f32[12,64]{1,0:T(8,128)} copy(f32[12,64]{1,0:T(8,128)S(1)} %scores.1) | data formatting | bytes 6144

commit v6 on v5

--- a/solution.py
+++ b/solution.py
@@ -152,15 +152,8 @@
         total = None
         for i in range(first, first + count):
             await_bytes(stages[i], load_sem.at[i])
-            tiles = stages[i].shape[0]
-            cuts = 2 if i >= LEFT_CHUNKS + RIGHT_CHUNKS - 2 else 1
-            terms = []
-            for c in range(cuts):
-                deep = jnp.concatenate(
-                    [stages[i][k] for k in range(c * tiles // cuts, (c + 1) * tiles // cuts)], axis=1
-                )
-                terms.append(dot_nt(deep[tokens:], deep[:tokens]))
-            term = sum(terms[1:], terms[0])
+            deep = jnp.concatenate([stages[i][k] for k in range(stages[i].shape[0])], axis=1)
+            term = dot_nt(deep[tokens:], deep[:tokens])
             total = term if total is None else total + term
         totals.append(total)
     left, right = totals

time: 18.3 us -> 18.3 us (level)
  no operation moved by 1% of the time
where the time goes in v6:
time: 18.3 us; the launch traced here: 18.1 us
  Pallas kernels  17.5 us (96%)
  local copies, waits for them, and re-layouts  0.6 us (3%)
    pallas_call x1, Pallas kernels, fused(): pl.pallas_call(functools.partial(score_kernel, n, cols, docs), name='scor...  17.5 us
    unnamed x1, local copies, waits for them, and re-layouts  0.6 us

profile of v6, /device:TPU:0, one launch (start us, length us, event | category | flops | bytes accessed | tf_op | source)
XLA Modules:
  0.0 18.1 jit_solution(3067412178598976471)
XLA Ops:
  0.0 17.5 %scores.1 = f32[12,64]{1,0:T(8,128)S(1)} custom-call(bf16[16,16,8,128]{3,2,1,0:T(8,128)(2,1)} %bitcast.19, bf16[16,56,8,128]{3,2,1,0:T(8,128)(2,1)} %bitcast.17, s32[1,128]{1,0:T(1,128)} %bitcast.21, bf16[8,16,8,128]{3,2,1,0:T(8,128)(2,1)} %bitcast.20, bf16[8,56,8,128]{3,2,1,0:T(8,128)(2,1)} %bitcast.18, f32[2048,512]{1,0:T(8,128)} %inv.1, ...), custom_call_target="tpu_custom_call" | custom-call | tf_op jit(solution)/shard_map/scores/pallas_call | solution.py:333
  17.5 0.6 %copy.9 = f32[12,64]{1,0:T(8,128)} copy(f32[12,64]{1,0:T(8,128)S(1)} %scores.1) | data formatting | bytes 6144
